TPU v7x, 32 devices: a 4x4x1 block of a 4x4x8 slice. The times are simulated.
32 devices in a mesh: rep: 2 (over z, core), dp: 16 (over x, y).
Axes of the slice: x: 4, y: 4, z: 1, core: 2. Of those that a mesh axis runs over, the one named last changes fastest.
The devices are a block of a 4x4x8 slice.
Arguments:
- x: bfloat16 [32, 4096, 768], P(('rep', 'dp')), parts along dimension 0
- dy: bfloat16 [32, 4096, 768], P(('rep', 'dp')), parts along dimension 0
- w_gate: bfloat16 [2, 768, 1792], P(None, 'dp')
- w_up: bfloat16 [2, 768, 1792], P(None, 'dp')
- w_down: bfloat16 [2, 1792, 768], P(None, 'dp')
- m_w_gate: float32 [2, 768, 1792], P(None, 'dp')
- m_w_up: float32 [2, 768, 1792], P(None, 'dp')
- m_w_down: float32 [2, 1792, 768], P(None, 'dp')
- v_w_gate: float32 [2, 768, 1792], P(None, 'dp')
- v_w_up: float32 [2, 768, 1792], P(None, 'dp')
- v_w_down: float32 [2, 1792, 768], P(None, 'dp')
Outputs:
- output 1: bfloat16 [4, 768, 1792], P('rep', 'dp'), parts along dimension 0
- output 2: bfloat16 [4, 768, 1792], P('rep', 'dp'), parts along dimension 0
- output 3: bfloat16 [4, 1792, 768], P('rep', 'dp'), parts along dimension 0
- output 4: float32 [4, 768, 1792], P('rep', 'dp'), parts along dimension 0
- output 5: float32 [4, 768, 1792], P('rep', 'dp'), parts along dimension 0
- output 6: float32 [4, 1792, 768], P('rep', 'dp'), parts along dimension 0
- output 7: float32 [4, 768, 1792], P('rep', 'dp'), parts along dimension 0
- output 8: float32 [4, 768, 1792], P('rep', 'dp'), parts along dimension 0
- output 9: float32 [4, 1792, 768], P('rep', 'dp'), parts along dimension 0
There are 2 independent parts. A program takes and returns all parts, laid end to end along the dimension named above; an argument that names none is the same for every part.
All inputs are finite; a program needn't handle non-finite values.
Results may differ from a plain program's by a relative error of at most 0.022.
Values are sent between devices in bfloat16 or wider.
A program may use at most 768 MiB of HBM per device.

v0:
```python
import jax
import jax.numpy as jnp
from jax import lax
from jax.sharding import PartitionSpec as P

NAMES = ("w_gate", "w_up", "w_down")


def matmul(a, w):
    return jnp.dot(a, w, preferred_element_type=jnp.float32).astype(jnp.bfloat16)


def normed(h):
    wide = h.astype(jnp.float32)
    scale = lax.rsqrt(jnp.mean(wide**2, -1, keepdims=True) + 1e-6)
    return (wide * scale).astype(jnp.bfloat16)


def layer(h, w):
    a = normed(h)
    gate = jnp.dot(a, w["w_gate"], preferred_element_type=jnp.float32)
    up = jnp.dot(a, w["w_up"], preferred_element_type=jnp.float32)
    return h + matmul((jax.nn.silu(gate) * up).astype(jnp.bfloat16), w["w_down"])


def adamw(w, m, v, g):
    m = 0.9 * m + 0.1 * g
    v = 0.95 * v + 0.05 * g * g
    step = m * lax.rsqrt(v + 1e-8) + 0.1 * w
    return (w - 0.02 * step).astype(jnp.bfloat16), m, v


def clipped(gradients, sum_of_squares, count):
    factor = jnp.minimum(1.0, 0.5 * lax.rsqrt(sum_of_squares / count + 1e-30))
    return [g * factor for g in gradients]


def solution(mesh):
    def fetched(weights, number):
        return {name: lax.all_gather(w[number], "dp", axis=0, tiled=True) for name, w in zip(NAMES, weights, strict=True)}

    def step(x, dy, *arrays):
        weights, m, v = (arrays[i : i + 3] for i in (0, 3, 6))
        layers = weights[0].shape[0]
        h, kept = x[0], []
        for number in range(layers):
            kept.append(h)
            h = layer(h, fetched(weights, number))
        by_h, mine = dy[0], [None] * layers
        for number in reversed(range(layers)):
            _, back = jax.vjp(lambda w, h: layer(h, w), fetched(weights, number), kept[number])
            by_w, by_h = back(by_h)
            mine[number] = [lax.psum_scatter(by_w[name], "dp", scatter_dimension=0, tiled=True) for name in NAMES]
        gradients = [jnp.stack([mine[number][i] for number in range(layers)]).astype(jnp.float32) for i in range(3)]
        squares = lax.psum(sum(jnp.sum(g * g) for g in gradients), "dp")
        gradients = clipped(gradients, squares, lax.psum(1, "dp") * sum(g.size for g in gradients))
        new = [adamw(w.astype(jnp.float32), m, v, g) for w, m, v, g in zip(weights, m, v, gradients, strict=True)]
        return tuple(one[which] for which in range(3) for one in new)

    states, cut = P(("rep", "dp"), None, None), P(None, "dp", None)
    return jax.shard_map(
        step,
        mesh=mesh,
        in_specs=(states, states) + (cut,) * 9,
        out_specs=(P("rep", "dp", None),) * 9,
        check_vma=False,
    )
```

profile of v0, /device:TPU:96, one launch (start us, length us, event | category | flops | bytes accessed | tf_op | source)
XLA Modules:
  0.0 851.1 jit_solution(3942586446493593137)
XLA Ops:
  7.3 1.8 fusion.102
  9.1 0.1 all-gather.15.cloned.1.call-start
  9.1 1.8 fusion.101
  11.0 0.1 all-gather.17.cloned.1.call-start
  11.0 1.8 fusion.100
  12.9 0.6 all-gather.23.cloned.1.call-update
  13.6 0.6 all-gather.21.cloned.1.call-update
  14.2 0.6 all-gather.19.cloned.1.call-update
  14.8 8.7 %copy.20 = bf16[1,4096,768]{1,2,0:T(8,128)(2,1)} copy(bf16[1,4096,768]{2,1,0:T(8,128)(2,1)} %param.11) | data formatting | bytes 12582912 | tf_op args[0]
  23.6 4.1 fusion.15
  27.7 8.7 %copy.21 = bf16[1,4096,768]{1,2,0:T(8,128)(2,1)} copy(bf16[1,4096,768]{2,1,0:T(8,128)(2,1)} %param.12) | data formatting | bytes 12582912 | tf_op args[1]
  36.3 18.2 %all-gather.13.cloned.1.call-done = bf16[1,768,1792]{2,1,0:T(8,128)(2,1)} async-done(((bf16[1,48,1792]{2,1,0:T(8,128)(2,1)}), bf16[1,768,1792]{2,1,0:T(8,128)(2,1)}) %all-gather.13.cloned.1.call-update) | async-done | bytes 2752528 | tf_op jit(solution)/shard_map/all_gather | solution.py:40
  54.5 19.8 %fusion.39 = f32[4096,1792]{1,0:T(8,128)} fusion(bf16[1,4096,768]{1,2,0:T(8,128)(2,1)} %copy.20, f32[4096]{0:T(1024)S(1)} %add_rsqrt_fusion, bf16[1,768,1792]{2,1,0:T(8,128)(2,1)} %all-gather.13.cloned.1.call-done), kind=kOutput, calls=%fused_computation.52 | convolution fusion | flops 11283726336 | bytes 38420480 | tf_op jit(solution)/shard_map/dot_general | solution.py:21
  74.3 23.3 %all-gather.15.cloned.1.call-done = bf16[1,768,1792]{2,1,0:T(8,128)(2,1)} async-done(((bf16[1,48,1792]{2,1,0:T(8,128)(2,1)}), bf16[1,768,1792]{2,1,0:T(8,128)(2,1)}) %all-gather.15.cloned.1.call-update) | async-done | bytes 2752528 | tf_op jit(solution)/shard_map/all_gather | solution.py:40
  97.7 33.7 %multiply_convert_fusion.1 = (bf16[4096,1792]{1,0:T(8,128)(2,1)}, f32[4096,1792]{1,0:T(8,128)}) fusion(f32[4096,1792]{1,0:T(8,128)} %fusion.39, bf16[1,768,1792]{2,1,0:T(8,128)(2,1)} %all-gather.15.cloned.1.call-done, bf16[1,4096,768]{1,2,0:T(8,128)(2,1)} %copy.20, f32[4096]{0:T(1024)S(1)} %add_rsqrt_fusion), kind=kOutput, calls=%fused_computation.17 | convolution fusion | flops 11327766528 | bytes 82460672 | tf_op jit(solution)/shard_map/dot_general | solution.py:22
  131.4 9.5 %all-gather.17.cloned.1.call-done = bf16[1,1792,768]{2,1,0:T(8,128)(2,1)} async-done(((bf16[1,112,768]{2,1,0:T(8,128)(2,1)}), bf16[1,1792,768]{2,1,0:T(8,128)(2,1)}) %all-gather.17.cloned.1.call-update) | async-done | bytes 2752528 | tf_op jit(solution)/shard_map/all_gather | solution.py:40
  140.8 19.1 %fusion.19 = (f32[4096]{0:T(1024)S(1)}, bf16[4096,768]{0,1:T(8,128)(2,1)}) fusion(bf16[4096,1792]{1,0:T(8,128)(2,1)} %get-tuple-element.24, bf16[1,1792,768]{2,1,0:T(8,128)(2,1)} %all-gather.17.cloned.1.call-done, bf16[1,4096,768]{1,2,0:T(8,128)(2,1)} %copy.20), kind=kOutput, calls=%fused_computation.37 | convolution fusion | flops 11290013696 | bytes 30031872 | tf_op jit(solution)/shard_map/dot_general | solution.py:10
  160.0 23.9 %all-gather.23.cloned.1.call-done = bf16[1,768,1792]{2,1,0:T(8,128)(2,1)} async-done(((bf16[1,48,1792]{2,1,0:T(8,128)(2,1)}), bf16[1,768,1792]{2,1,0:T(8,128)(2,1)}) %all-gather.23.cloned.1.call-update) | async-done | bytes 2752528 | tf_op jit(solution)/shard_map/all_gather | solution.py:40
  183.8 19.9 %fusion.31 = f32[4096,1792]{1,0:T(8,128)} fusion(bf16[4096,768]{0,1:T(8,128)(2,1)} %get-tuple-element.27, f32[4096]{0:T(1024)S(1)} %fusion.88, bf16[1,768,1792]{2,1,0:T(8,128)(2,1)} %all-gather.23.cloned.1.call-done), kind=kOutput, calls=%fused_computation.49 | convolution fusion | flops 11283726336 | bytes 38420480 | tf_op jit(solution)/shard_map/jvp()/dot_general | solution.py:22
  203.8 23.1 %all-gather.21.cloned.1.call-done = bf16[1,1792,768]{2,1,0:T(8,128)(2,1)} async-done(((bf16[1,112,768]{2,1,0:T(8,128)(2,1)}), bf16[1,1792,768]{2,1,0:T(8,128)(2,1)}) %all-gather.21.cloned.1.call-update) | async-done | bytes 2752528 | tf_op jit(solution)/shard_map/all_gather | solution.py:40
  226.8 17.5 %convolution_convert_fusion.1 = bf16[4096,1792]{1,0:T(8,128)(2,1)} fusion(bf16[1,4096,768]{2,1,0:T(8,128)(2,1)} %param.12, bf16[1,1792,768]{2,1,0:T(8,128)(2,1)} %all-gather.21.cloned.1.call-done), kind=kOutput, calls=%fused_computation.30 | convolution fusion | flops 11281629184 | bytes 23724032 | tf_op jit(solution)/shard_map/transpose(jvp())/dot_general | solution.py:10
  244.4 25.5 %all-gather.19.cloned.1.call-done = bf16[1,768,1792]{2,1,0:T(8,128)(2,1)} async-done(((bf16[1,48,1792]{2,1,0:T(8,128)(2,1)}), bf16[1,768,1792]{2,1,0:T(8,128)(2,1)}) %all-gather.19.cloned.1.call-update) | async-done | bytes 2752528 | tf_op jit(solution)/shard_map/all_gather | solution.py:40
  269.9 39.9 %fusion.2 = (bf16[4096,1792]{1,0:T(8,128)(2,1)}, f32[4096,1792]{1,0:T(8,128)}) fusion(f32[4096,1792]{1,0:T(8,128)} %fusion.31, bf16[4096,1792]{1,0:T(8,128)(2,1)} %convolution_convert_fusion.1, bf16[1,768,1792]{2,1,0:T(8,128)(2,1)} %all-gather.19.cloned.1.call-done, bf16[4096,768]{0,1:T(8,128)(2,1)} %get-tuple-element.27, f32[4096]{0:T(1024)S(1)} %fusion.88), kind=kOutput, calls=%fused_computation.8 | convolution fusion | flops 11371806720 | bytes 97140736 | tf_op jit(solution)/shard_map/jvp()/dot_general | solution.py:21
  309.8 18.8 %fusion.49 = bf16[768,1792]{1,0:T(8,128)(2,1)} fusion(bf16[4096,1792]{1,0:T(8,128)(2,1)} %get-tuple-element.28, bf16[4096,768]{0,1:T(8,128)(2,1)} %get-tuple-element.27, f32[4096]{0:T(1024)S(1)} %fusion.88), kind=kOutput, calls=%fused_computation.56 | convolution fusion | flops 11283726336 | bytes 23740416 | tf_op jit(solution)/shard_map/transpose(jvp())/dot_general | solution.py:21
  328.6 0.1 reduce-scatter.7.cloned.1.call-start
  328.7 23.5 %fusion.22 = bf16[4096,768]{0,1:T(8,128)(2,1)} fusion(bf16[4096,1792]{1,0:T(8,128)(2,1)} %convolution_convert_fusion.1, bf16[1,768,1792]{2,1,0:T(8,128)(2,1)} %all-gather.23.cloned.1.call-done, f32[4096,1792]{1,0:T(8,128)} %get-tuple-element.29), kind=kOutput, calls=%fused_computation.40 | convolution fusion | flops 11321475072 | bytes 53084160 | tf_op jit(solution)/shard_map/transpose(jvp())/dot_general | solution.py:22
  352.2 20.4 %fusion.21 = (f32[4096]{0:T(1024)S(1)}, bf16[4096,768]{0,1:T(8,128)(2,1)}) fusion(bf16[4096,768]{0,1:T(8,128)(2,1)} %get-tuple-element.27, bf16[4096,768]{0,1:T(8,128)(2,1)} %fusion.22, bf16[4096,1792]{1,0:T(8,128)(2,1)} %get-tuple-element.28, bf16[1,768,1792]{2,1,0:T(8,128)(2,1)} %all-gather.19.cloned.1.call-done), kind=kOutput, calls=%fused_computation.39 | convolution fusion | flops 11290013696 | bytes 36323328 | tf_op jit(solution)/shard_map/transpose(jvp())/dot_general | solution.py:21
  372.7 9.7 %fusion.23 = bf16[4096,768]{0,1:T(8,128)(2,1)} fusion(bf16[4096,768]{0,1:T(8,128)(2,1)} %get-tuple-element.27, bf16[4096,768]{0,1:T(8,128)(2,1)} %get-tuple-element.31, bf16[1,4096,768]{1,2,0:T(8,128)(2,1)S(1)} %bitcast.69, f32[4096]{0:T(1024)S(1)} %multiply_multiply_fusion.3, f32[4096]{0:T(1024)S(1)} %fusion.88), kind=kLoop, calls=%fused_computation.43 | loop fusion | flops 22020096 | bytes 25198592 | tf_op jit(solution)/shard_map/transpose(jvp())/add_any | solution.py:14
  382.3 19.7 %convolution_convert_fusion = bf16[4096,1792]{1,0:T(8,128)(2,1)} fusion(bf16[4096,768]{0,1:T(8,128)(2,1)} %fusion.23, bf16[1,1792,768]{2,1,0:T(8,128)(2,1)S(1)} %copy-done.10), kind=kOutput, calls=%fused_computation.29 | convolution fusion | flops 11281629184 | bytes 23724032 | tf_op jit(solution)/shard_map/transpose(jvp())/dot_general | solution.py:10
  402.0 29.9 %fusion.41 = bf16[768,1792]{1,0:T(8,128)(2,1)} fusion(f32[4096,1792]{1,0:T(8,128)} %fusion.39, f32[4096,1792]{1,0:T(8,128)} %get-tuple-element.25, bf16[4096,1792]{1,0:T(8,128)(2,1)} %convolution_convert_fusion, bf16[1,4096,768]{1,2,0:T(8,128)(2,1)} %copy.20, f32[4096]{0:T(1024)S(1)} %copy-done.9), kind=kOutput, calls=%fused_computation.53 | convolution fusion | flops 11365842944 | bytes 82460672 | tf_op jit(solution)/shard_map/transpose(jvp())/dot_general | solution.py:21
  432.0 0.1 reduce-scatter.13.cloned.1.call-start
  432.1 25.3 %fusion.55 = bf16[768,1792]{1,0:T(8,128)(2,1)} fusion(bf16[4096,1792]{1,0:T(8,128)(2,1)} %convolution_convert_fusion.1, bf16[4096,768]{0,1:T(8,128)(2,1)} %get-tuple-element.27, f32[4096]{0:T(1024)S(1)} %fusion.88, f32[4096,1792]{1,0:T(8,128)} %get-tuple-element.29), kind=kOutput, calls=%fused_computation.58 | convolution fusion | flops 11329142784 | bytes 53100544 | tf_op jit(solution)/shard_map/transpose(jvp())/dot_general | solution.py:22
  457.5 0.1 reduce-scatter.11.cloned.1.call-start
  457.6 25.1 %fusion.46 = bf16[768,1792]{1,0:T(8,128)(2,1)} fusion(bf16[4096,1792]{1,0:T(8,128)(2,1)} %convolution_convert_fusion, f32[4096,1792]{1,0:T(8,128)} %fusion.39, bf16[1,4096,768]{1,2,0:T(8,128)(2,1)} %copy.20, f32[4096]{0:T(1024)S(1)} %copy-done.9), kind=kOutput, calls=%fused_computation.54 | convolution fusion | flops 11329142784 | bytes 53100544 | tf_op jit(solution)/shard_map/transpose(jvp())/dot_general | solution.py:22
  482.7 0.1 reduce-scatter.17.cloned.1.call-start
  482.8 26.3 %fusion.52 = bf16[1792,768]{1,0:T(8,128)(2,1)} fusion(bf16[1,4096,768]{2,1,0:T(8,128)(2,1)} %param.12, f32[4096,1792]{1,0:T(8,128)} %fusion.31, f32[4096,1792]{1,0:T(8,128)} %get-tuple-element.29), kind=kOutput, calls=%fused_computation.57 | convolution fusion | flops 11319705600 | bytes 67764224 | tf_op jit(solution)/shard_map/transpose(jvp())/dot_general | solution.py:10
  509.2 0.1 reduce-scatter.15.cloned.1.call-start
  509.3 17.9 %convolution_convert_fusion.4 = bf16[1792,768]{1,0:T(8,128)(2,1)} fusion(bf16[4096,1792]{1,0:T(8,128)(2,1)} %get-tuple-element.24, bf16[4096,768]{0,1:T(8,128)(2,1)} %fusion.23), kind=kOutput, calls=%fused_computation.55 | convolution fusion | flops 11275665408 | bytes 23724032 | tf_op jit(solution)/shard_map/transpose(jvp())/dot_general | solution.py:10
  527.3 1.8 fusion.76
  529.1 46.9 %reduce-scatter.13.cloned.1.call-done = bf16[48,1792]{1,0:T(8,128)(2,1)} async-done(((bf16[768,1792]{1,0:T(8,128)(2,1)}), bf16[48,1792]{1,0:T(8,128)(2,1)}) %reduce-scatter.13.cloned.1.call-update) | async-done | bytes 172048 | tf_op jit(solution)/shard_map/reduce_scatter | solution.py:53
  576.0 73.3 %reduce-scatter.11.cloned.1.call-done = bf16[48,1792]{1,0:T(8,128)(2,1)} async-done(((bf16[768,1792]{1,0:T(8,128)(2,1)}), bf16[48,1792]{1,0:T(8,128)(2,1)}) %reduce-scatter.11.cloned.1.call-update) | async-done | bytes 172048 | tf_op jit(solution)/shard_map/reduce_scatter | solution.py:53
  649.3 1.8 fusion.77
  652.4 70.4 %reduce-scatter.17.cloned.1.call-done = bf16[112,768]{1,0:T(8,128)(2,1)} async-done(((bf16[1792,768]{1,0:T(8,128)(2,1)}), bf16[112,768]{1,0:T(8,128)(2,1)}) %reduce-scatter.17.cloned.1.call-update) | async-done | bytes 172048 | tf_op jit(solution)/shard_map/reduce_scatter | solution.py:53
  722.8 73.3 %reduce-scatter.15.cloned.1.call-done = bf16[112,768]{1,0:T(8,128)(2,1)} async-done(((bf16[1792,768]{1,0:T(8,128)(2,1)}), bf16[112,768]{1,0:T(8,128)(2,1)}) %reduce-scatter.15.cloned.1.call-update) | async-done | bytes 172048 | tf_op jit(solution)/shard_map/reduce_scatter | solution.py:53
  796.0 1.8 fusion.78
  798.5 38.7 %psum.7 = f32[]{:T(128)} all-reduce(f32[]{:T(128)S(6)} %add.99), channel_id=1, replica_groups=mesh['rep'=2,'dp'=16] {'dp'}, use_global_device_ids=true, to_apply=%region_12.13 | all-reduce | flops 1 | bytes 8 | tf_op jit(solution)/shard_map/psum | solution.py:55
  837.9 2.4 fusion.84
  840.2 3.9 fusion.75
  (46 shorter events, 0.9 us)
Async XLA Ops:
  7.2 47.3 %all-gather.13.cloned.1.call-start = ((), (), s32[]{:S(2)}) async-start(), calls=%async_computation.12 | async-start | bytes 2924544 | tf_op jit(solution)/shard_map/all_gather | solution.py:40
  9.1 88.6 %all-gather.15.cloned.1.call-start = ((), (), s32[]{:S(2)}) async-start(), calls=%async_computation.13 | async-start | bytes 2924544 | tf_op jit(solution)/shard_map/all_gather | solution.py:40
  11.0 129.9 %all-gather.17.cloned.1.call-start = ((), (), s32[]{:S(2)}) async-start(), calls=%async_computation.14 | async-start | bytes 2924544 | tf_op jit(solution)/shard_map/all_gather | solution.py:40
  12.8 171.0 %all-gather.23.cloned.1.call-start = ((), (), s32[]{:S(2)}) async-start(), calls=%async_computation.17 | async-start | bytes 2924544 | tf_op jit(solution)/shard_map/all_gather | solution.py:40
  13.5 213.4 %all-gather.21.cloned.1.call-start = ((), (), s32[]{:S(2)}) async-start(), calls=%async_computation.16 | async-start | bytes 2924544 | tf_op jit(solution)/shard_map/all_gather | solution.py:40
  14.1 255.7 %all-gather.19.cloned.1.call-start = ((), (), s32[]{:S(2)}) async-start(), calls=%async_computation.15 | async-start | bytes 2924544 | tf_op jit(solution)/shard_map/all_gather | solution.py:40
  14.8 512.5 %reduce-scatter.9.cloned.1.call-start = ((), (), s32[]{:S(2)}) async-start(), calls=%async_computation.7 | async-start | bytes 2924544 | tf_op jit(solution)/shard_map/reduce_scatter | solution.py:53
  27.7 70.0 %copy-start.8 = (f32[4096]{0:T(1024)}, f32[4096]{0:T(1024)S(1)}, u32[]{:S(2)}) copy-start(f32[4096]{0:T(1024)S(1)} %add_rsqrt_fusion) | copy-start | bytes 49156
  160.0 43.8 %copy-start.6 = (f32[4096]{0:T(1024)}, f32[4096]{0:T(1024)S(1)}, u32[]{:S(2)}) copy-start(f32[4096]{0:T(1024)S(1)} %get-tuple-element.26) | copy-start | bytes 49156
  309.8 62.8 %slice-start = ((s8[6291456]{0:T(1024)(128)(4,1)}), s8[2097152]{0:T(1024)(128)(4,1)S(1)}, s32[]{:S(2)}) async-start(s8[6291456]{0:T(1024)(128)(4,1)} %bitcast.68), calls=%async_computation.18 | async-start | bytes 4194304
  328.6 198.7 %reduce-scatter.7.cloned.1.call-start = ((), (), s32[]{:S(2)}) async-start(), calls=%async_computation.6 | async-start | bytes 2924544 | tf_op jit(solution)/shard_map/reduce_scatter | solution.py:53
  328.7 44.0 %slice-start.1 = ((s8[6291456]{0:T(1024)(128)(4,1)}), s8[4194304]{0:T(1024)(128)(4,1)S(1)}, s32[]{:S(2)}) async-start(s8[6291456]{0:T(1024)(128)(4,1)} %bitcast.68), calls=%async_computation.19 | async-start | bytes 8388608
  352.2 20.4 %copy-start.7 = (f32[4096]{0:T(1024)S(1)}, f32[4096]{0:T(1024)}, u32[]{:S(2)}) copy-start(f32[4096]{0:T(1024)} %copy-done.6) | copy-start | bytes 49156
  372.7 9.7 %copy-start.10 = (bf16[1,1792,768]{2,1,0:T(8,128)(2,1)S(1)}, bf16[1,1792,768]{2,1,0:T(8,128)(2,1)}, u32[]{:S(2)}) copy-start(bf16[1,1792,768]{2,1,0:T(8,128)(2,1)} %all-gather.17.cloned.1.call-done) | copy-start | bytes 8257540
  382.3 19.7 %copy-start.9 = (f32[4096]{0:T(1024)S(1)}, f32[4096]{0:T(1024)}, u32[]{:S(2)}) copy-start(f32[4096]{0:T(1024)} %copy-done.8) | copy-start | bytes 49156
  432.0 144.0 %reduce-scatter.13.cloned.1.call-start = ((), (), s32[]{:S(2)}) async-start(), calls=%async_computation.9 | async-start | bytes 2924544 | tf_op jit(solution)/shard_map/reduce_scatter | solution.py:53
  457.5 191.8 %reduce-scatter.11.cloned.1.call-start = ((), (), s32[]{:S(2)}) async-start(), calls=%async_computation.8 | async-start | bytes 2924544 | tf_op jit(solution)/shard_map/reduce_scatter | solution.py:53
  482.7 240.0 %reduce-scatter.17.cloned.1.call-start = ((), (), s32[]{:S(2)}) async-start(), calls=%async_computation.11 | async-start | bytes 2924544 | tf_op jit(solution)/shard_map/reduce_scatter | solution.py:53
  509.1 328.7 %copy-start = (bf16[2,112,768]{2,1,0:T(8,128)(2,1)S(1)}, bf16[2,112,768]{2,1,0:T(8,128)(2,1)}, u32[]{:S(2)}) copy-start(bf16[2,112,768]{2,1,0:T(8,128)(2,1)} %param.15) | copy-start | bytes 1032196
  509.1 328.7 %copy-start.3 = (f32[2,112,768]{2,1,0:T(8,128)S(1)}, f32[2,112,768]{2,1,0:T(8,128)}, u32[]{:S(2)}) copy-start(f32[2,112,768]{2,1,0:T(8,128)} %param.21) | copy-start | bytes 2064388
  509.2 328.7 %copy-start.4 = (f32[2,112,768]{2,1,0:T(8,128)S(1)}, f32[2,112,768]{2,1,0:T(8,128)}, u32[]{:S(2)}) copy-start(f32[2,112,768]{2,1,0:T(8,128)} %param.18) | copy-start | bytes 2064388
  509.2 331.1 %copy-start.1 = (bf16[2,48,1792]{2,1,0:T(8,128)(2,1)S(1)}, bf16[2,48,1792]{2,1,0:T(8,128)(2,1)}, u32[]{:S(2)}) copy-start(bf16[2,48,1792]{2,1,0:T(8,128)(2,1)} %param.13) | copy-start | bytes 1032196
  509.2 331.1 %copy-start.2 = (bf16[2,48,1792]{2,1,0:T(8,128)(2,1)S(1)}, bf16[2,48,1792]{2,1,0:T(8,128)(2,1)}, u32[]{:S(2)}) copy-start(bf16[2,48,1792]{2,1,0:T(8,128)(2,1)} %param.14) | copy-start | bytes 1032196
  509.2 331.0 %copy-start.5 = (f32[2,48,1792]{2,1,0:T(8,128)S(1)}, f32[2,48,1792]{2,1,0:T(8,128)}, u32[]{:S(2)}) copy-start(f32[2,48,1792]{2,1,0:T(8,128)} %param.19) | copy-start | bytes 2064388
  509.2 286.8 %reduce-scatter.15.cloned.1.call-start = ((), (), s32[]{:S(2)}) async-start(), calls=%async_computation.10 | async-start | bytes 2924544 | tf_op jit(solution)/shard_map/reduce_scatter | solution.py:53
Sparse Core Ops, SparseCore 0:
  10.6 43.8 all-gather.12
  57.1 40.5 all-gather.14
  100.2 40.5 all-gather.16
  143.3 40.5 all-gather.22
  186.3 40.5 all-gather.20
  229.3 40.5 all-gather.18
  328.7 70.2 reduce-scatter.8
  432.1 70.2 reduce-scatter.6
  505.6 70.3 reduce-scatter.12
  579.0 70.2 reduce-scatter.10
  652.4 70.2 reduce-scatter.16
  725.8 70.2 reduce-scatter.14
where the time goes:
time: 859 us; the launch traced here: 851 us
  waiting for transfers between devices  389 us (45%)
  matrix products  357 us (42%)
  blocking collectives  38.7 us (5%)
  other arithmetic  25.4 us (3%)
  local copies, waits for them, and re-layouts  22.7 us (3%)
  between operations  17.2 us (2%)
    reduce_scatter x6, waiting for transfers between devices, step(): lax.psum_scatter(by_w[name], 'dp', scatter_dimension=0, tiled=True)  264 us
    dot_general x5, matrix products, layer(): gate = jnp.dot(a, w['w_gate'], preferred_element_type=jnp.float32)  129 us
    dot_general x5, matrix products, layer(): up = jnp.dot(a, w['w_up'], preferred_element_type=jnp.float32)  128 us
    all_gather x6, waiting for transfers between devices, fetched(): lax.all_gather(w[number], 'dp', axis=0, tiled=True)  123 us
    dot_general x5, matrix products, matmul(): jnp.dot(a, w, preferred_element_type=jnp.float32).astype(jnp.bfloat16)  101 us
    psum x1, blocking collectives, step(): squares = lax.psum(sum((jnp.sum(g * g) for g in gradients)), 'dp')  38.7 us
    unnamed x28, local copies, waits for them, and re-layouts  17.4 us
  transfers between devices with their start and end apart: 12, of which 10 were waited for; matrix products, arithmetic and copies ran while one was open for 40% of the time, Pallas kernels for 0%

commit v1 on v0

v1 whole, which is shorter than its diff:
```python
import functools
import math

import jax
import jax.numpy as jnp
from jax import lax
from jax.experimental import pallas as pl
from jax.experimental.pallas import tpu as pltpu
from jax.sharding import PartitionSpec as P

BF16, F32 = jnp.bfloat16, jnp.float32
LANES = 128
CHUNK = 2 * LANES
TILE = 256
UNROLL = 4
SPAN = TILE * UNROLL
WIDE = 512
EPS = 1e-6
BOTH = (0, 1)
ANY = pl.BlockSpec(memory_space=pl.ANY)
VMEM = pl.BlockSpec(memory_space=pltpu.VMEM)
MESH_IDS = pl.DeviceIdType.MESH
VMEM_LIMIT = 67_000_000


def dot(a, b):
    return jnp.dot(a, b, preferred_element_type=F32)


def dot_nt(a, b):
    return lax.dot_general(a, b, (((1,), (1,)), ((), ())), preferred_element_type=F32)


def rounded(x):
    return x.astype(BF16).astype(F32)


def aligned(start, size):
    return pl.ds(pl.multiple_of(start, size), size)


def local(src, dst, sem):
    return pltpu.make_async_copy(src, dst, sem)


def loop(n, body):
    def step(i, carry):
        body(i)
        return carry

    lax.fori_loop(0, n, step, 0)


class Torus:
    def __init__(self, side):
        index = lax.axis_index("dp")
        self.side = side
        self.at = (index // side, lax.rem(index, side))

    def near(self, axis, away):
        return lax.rem(self.at[axis] + away + self.side, self.side)

    def id(self, axis, away):
        place = [self.at[0], self.at[1]]
        place[axis] = self.near(axis, away)
        return {"dp": place[0] * self.side + place[1]}

    def partner(self):
        rep = lax.axis_index("rep")
        return {"rep": rep + 1 - 2 * lax.rem(rep, 2)}

    def greet(self, targets):
        barrier = pltpu.get_barrier_semaphore()
        for target in targets:
            pl.semaphore_signal(barrier, inc=1, device_id=target, device_id_type=MESH_IDS)
        pl.semaphore_wait(barrier, len(targets))


def remote(src, dst, send, recv, target):
    return pltpu.make_async_remote_copy(src_ref=src, dst_ref=dst, send_sem=send, recv_sem=recv, device_id=target, device_id_type=MESH_IDS)


class Gather:
    def __init__(self, torus, full, own, sems):
        self.t, self.full, self.own, self.send, self.recv = torus, full, own, sems.at[0], sems.at[1]
        self.core = lax.rem(lax.axis_index("rep"), 2)

    def cols(self, piece):
        return aligned(piece * CHUNK + self.core * LANES, LANES)

    def copy(self, k, which, src, dst, target):
        return remote(src, dst, self.send.at[k, which], self.recv.at[k, which], target)

    def block(self, axis, along, piece):
        i = (along, self.t.at[1]) if axis == 0 else (self.t.at[0], along)
        return self.full.at[i[0], i[1], :, self.cols(piece)]

    def line(self, axis, across, piece):
        c = self.cols(piece)
        return self.full.at[:, across, :, c] if axis == 0 else self.full.at[across, :, :, c]

    def near_pair(self, k, piece, axis):
        b = self.block(axis, self.t.at[axis], piece)
        own = self.own.at[:, self.cols(piece)]
        return [self.copy(k, n, own, b, self.t.id(axis, 1 - 2 * n)) for n in BOTH]

    def far_block(self, k, piece, axis, odd):
        b = self.block(axis, self.t.near(axis, 2 * odd - 1), piece)
        return self.copy(k, 2, b, b, self.t.id(axis, 1 - 2 * odd))

    def line_pair(self, k, piece, axis):
        mine = self.line(axis, self.t.at[1 - axis], piece)
        return [self.copy(k, 3 + n, mine, mine, self.t.id(1 - axis, 1 - 2 * n)) for n in BOTH]

    def far_line(self, k, piece, axis, odd):
        line = self.line(axis, self.t.near(1 - axis, 2 * odd - 1), piece)
        return self.copy(k, 5, line, line, self.t.id(1 - axis, 1 - 2 * odd))

    def across(self, k, piece):
        whole = self.full.at[:, :, :, self.cols(piece)]
        return self.copy(k, 6, whole, whole, self.t.partner())

    def wait(self, k, which, like):
        self.copy(k, which, like, like, self.t.partner()).wait_recv()

    def stage(self, n, k, piece, axis, odd):
        block = self.block(axis, self.t.at[axis], piece)
        line = self.line(axis, self.t.at[1 - axis], piece)
        if n == 0:
            for c in self.near_pair(k, piece, axis):
                c.start()
        elif n == 1:
            self.wait(k, odd, block)
            self.far_block(k, piece, axis, odd).start()
        elif n == 2:
            self.wait(k, 1 - odd, block)
            self.wait(k, 2, block)
            for c in self.line_pair(k, piece, axis):
                c.start()
        elif n == 3:
            self.wait(k, 3 + odd, line)
            self.far_line(k, piece, axis, odd).start()
        elif n == 4:
            self.wait(k, 4 - odd, line)
            self.wait(k, 5, line)
            self.across(k, piece).start()
        elif n == 5:
            self.wait(k, 6, self.full.at[:, :, :, self.cols(piece)])
        else:
            for c in self.near_pair(k, piece, axis) + self.line_pair(k, piece, axis):
                c.wait_send()
            self.far_block(k, piece, axis, odd).wait_send()
            self.far_line(k, piece, axis, odd).wait_send()
            self.across(k, piece).wait_send()


class Scatter:
    def __init__(self, torus, rows, refs):
        self.t, self.rows = torus, rows
        self.sa, self.ra, self.sb, self.rb, self.q, self.sems = refs

    @staticmethod
    def scratch(side, rows, pieces, slots):
        return [
            pltpu.VMEM((slots, 3, side, rows, LANES), BF16),
            pltpu.VMEM((pieces, 3, side, rows, LANES), BF16),
            pltpu.VMEM((slots, 3, rows, LANES), BF16),
            pltpu.VMEM((pieces, 3, rows, LANES), BF16),
            pltpu.VMEM((slots, side, rows, LANES), F32),
            pltpu.SemaphoreType.DMA((pieces, 2, 2, 3)),
        ]

    def copy(self, phase, k, slot, which, axis, way):
        src, dst = ((self.sa, self.ra), (self.sb, self.rb))[phase]
        if phase:
            axis = 1 - axis
        target = self.t.id(axis, -way if which == 1 else way)
        sems = self.sems.at[k, phase]
        return remote(src.at[slot, which], dst.at[k, which], sems.at[0, which], sems.at[1, which], target)

    def stage(self, n, k, slot, axis, way, own, out):
        t, side, other = self.t, self.t.side, 1 - axis

        def term(along, across):
            return own(along, across) if axis == 0 else own(across, along)

        if n == 0:
            for which, away in ((0, 2), (1, -way)):
                for i in range(side):
                    self.sa[slot, which, i] = term(t.near(axis, away), i).astype(BF16)
                self.copy(0, k, slot, which, axis, way).start()
        elif n == 1:
            self.copy(0, k, slot, 0, axis, way).wait_recv()
            for i in range(side):
                self.sa[slot, 2, i] = (term(t.near(axis, way), i) + self.ra[k, 0, i].astype(F32)).astype(BF16)
            self.copy(0, k, slot, 2, axis, way).start()
        elif n == 2:
            for which in (1, 2):
                self.copy(0, k, slot, which, axis, way).wait_recv()
            for i in range(side):
                self.q[slot, i] = term(t.at[axis], i) + self.ra[k, 1, i].astype(F32) + self.ra[k, 2, i].astype(F32)
            for which, away in ((0, 2), (1, -way)):
                self.sb[slot, which] = self.q[slot, t.near(other, away)].astype(BF16)
                self.copy(1, k, slot, which, axis, way).start()
        elif n == 3:
            self.copy(1, k, slot, 0, axis, way).wait_recv()
            self.sb[slot, 2] = (self.q[slot, t.near(other, way)] + self.rb[k, 0].astype(F32)).astype(BF16)
            self.copy(1, k, slot, 2, axis, way).start()
        else:
            for which in (1, 2):
                self.copy(1, k, slot, which, axis, way).wait_recv()
            out(self.q[slot, t.at[other]] + self.rb[k, 1].astype(F32) + self.rb[k, 2].astype(F32))
            for phase in BOTH:
                for which in range(3):
                    self.copy(phase, k, slot, which, axis, way).wait_send()


def greeted(t, aways):
    return [t.id(axis, away) for axis in BOTH for away in aways]


def scale_of(wide):
    return lax.rsqrt(jnp.mean(wide * wide, -1, keepdims=True) + EPS)


def normed(h):
    wide = h.astype(F32)
    return (wide * scale_of(wide)).astype(BF16)


def front_kernel(side, x, dy, wg, wu, wd, ao, bo, po, a0t, dyt, ho, a1, a1t, wd0o, wg1, wu1, wd1, vx, va, vp, vg, vu, vd, ab, td, tt, th, ta, xsem, psem, asem, sem, *gather_sems):
    t = Torus(side)
    tokens, ff = vp.shape
    d = vx.shape[1]
    chunks, dchunks, blocks, spans = ff // CHUNK, d // CHUNK, tokens // WIDE, tokens // SPAN
    me = t.at

    def rows_of(b):
        return aligned(b * WIDE, WIDE)

    def xin(b):
        return local(x.at[rows_of(b)], vx.at[rows_of(b)], xsem.at[b])

    loop(blocks, lambda b: xin(b).start())
    for full, shard in ((vg, wg), (vu, wu), (vd, wd)):
        full[me[0], me[1]] = shard[0]
    own1 = [local(s.at[1], o.at[me[0], me[1]], psem.at[i]) for i, (s, o) in enumerate(((wg, wg1), (wu, wu1), (wd, wd1)))]
    for c in own1:
        c.start()
    t.greet([*greeted(t, (1, -1)), t.partner()])

    shards, layers = (wg, wu, wd), ((vg, vu, vd), (wg1, wu1, wd1))
    gathers = [[Gather(t, f, s.at[n], gather_sems[3 * n + i]) for i, (f, s) in enumerate(zip(fulls, shards))] for n, fulls in enumerate(layers)]

    def wide(layer, n, c):
        for axis in BOTH:
            gathers[layer][axis].stage(n, c, c, axis, lax.rem(c, 2))

    def tall(layer, n):
        for c in range(dchunks):
            gathers[layer][2].stage(n, c, c, (c + layer) % 2, (c // 2 + layer) % 2)

    def all_wide(layer, n):
        loop(chunks, lambda c: wide(layer, n, c))

    def due(i, plan):
        for at, *work in plan:

            @pl.when(i == at)
            def _(work=work):
                for f, *args in work:
                    f(*args)

    all_wide(0, 0)

    def turned(dst, b):
        slot = lax.rem(b, 2)
        return local(tt.at[slot], dst.at[:, rows_of(b)], sem.at[slot])

    def turn(dst, plan, get):
        def block(b):
            @pl.when(b >= 2)
            def _():
                turned(dst, b).wait()

            for q in range(0, WIDE, LANES):
                tt[lax.rem(b, 2), :, pl.ds(q, LANES)] = get(b, q).T
            turned(dst, b).start()
            due(b, plan)

        loop(blocks, block)
        for b in BOTH:
            turned(dst, b).wait()

    def first_states(b, q):
        if q == 0:
            xin(b).wait()
        r = aligned(b * WIDE + q, LANES)
        a = normed(vx[r, :])
        va[r, :] = a
        return a

    def dyin(b):
        slot = lax.rem(b, 2)
        return local(dy.at[rows_of(b)], td.at[slot], sem.at[2 + slot])

    def cotangent(b, q):
        if q == 0:

            @pl.when(b + 1 < blocks)
            def _():
                dyin(b + 1).start()

            dyin(b).wait()
        return td[lax.rem(b, 2), pl.ds(q, LANES), :]

    dyin(0).start()
    turn(a0t, ((2, (all_wide, 0, 1)), (6, (all_wide, 0, 2), (tall, 0, 0))), first_states)
    turn(dyt, ((2, (wide, 0, 3, 0)), (6, (wide, 0, 4, 0), (wide, 0, 3, 1))), cotangent)
    for c in own1:
        c.wait()

    def saved(c, j):
        return [local(ab.at[i, j], dst.at[c, aligned(j * SPAN, SPAN)], asem.at[i, j]) for i, dst in enumerate((ao, bo))]

    def kept(c):
        return local(vp.at[:, aligned(c * CHUNK, CHUNK)], po.at[c], psem.at[c])

    def hidden(c):
        for n in (3, 4, 5):

            @pl.when(c + (5 - n) < chunks)
            def _(n=n):
                wide(0, n, c + (5 - n))

        due(c, ((0, (tall, 0, 1), (all_wide, 1, 0)), (1, (tall, 0, 2)), (2, (tall, 0, 3), (all_wide, 1, 1)), (3, (tall, 1, 0))))
        due(c, ((4, (tall, 0, 4), (all_wide, 1, 2)), (5, (tall, 1, 1)), (6, (tall, 1, 2), (all_wide, 1, 3))))
        cols = aligned(c * CHUNK, CHUNK)

        def span(j):
            @pl.when(c >= 1)
            def _():
                for copy in saved(c, j):
                    copy.wait()

            for u in range(UNROLL):
                r = aligned(j * SPAN + u * TILE, TILE)
                a = va[r, :]
                gate = dot(a, vg[:, :, :, cols].reshape(d, CHUNK))
                up = dot(a, vu[:, :, :, cols].reshape(d, CHUNK))
                s = 1 / (1 + jnp.exp(-gate))
                b = gate * s
                mine = pl.ds(u * TILE, TILE)
                ab[0, j, mine, :] = up * (s + b * (1 - s))
                ab[1, j, mine, :] = b
                vp[r, cols] = (b * up).astype(BF16)
            for copy in saved(c, j):
                copy.start()

        loop(spans, span)
        kept(c).start()

    loop(chunks, hidden)
    for j in range(spans):
        for copy in saved(0, j):
            copy.wait()
    tall(0, 5)
    dcopy = local(vd, wd0o, xsem.at[0])
    dcopy.start()

    def outs(b):
        s = lax.rem(b, 2)
        r = rows_of(b)
        pairs = ((th, ho.at[r]), (ta, a1.at[r]), (tt, a1t.at[:, r]))
        return [local(src.at[s], dst, sem.at[2 * i + s]) for i, (src, dst) in enumerate(pairs)]

    def down(b):
        due(b, ((1, (tall, 1, 3)), (2, (all_wide, 1, 4)), (4, (tall, 1, 4))))

        @pl.when(b >= 2)
        def _():
            for c in outs(b):
                c.wait()

        s = lax.rem(b, 2)
        r = rows_of(b)
        h = (vx[r, :].astype(F32) + rounded(dot(vp[r, :], vd[...].reshape(ff, d)))).astype(BF16)
        a = normed(h)
        th[s] = h
        ta[s] = a
        tt[s] = a.T
        for c in outs(b):
            c.start()

    loop(blocks, down)
    for b in BOTH:
        for c in outs(b):
            c.wait()
    loop(chunks, lambda c: kept(c).wait())
    dcopy.wait()
    all_wide(1, 5)
    tall(1, 5)
    for layer in BOTH:
        all_wide(layer, 6)
        tall(layer, 6)


def front(side, x, dy, wg, wu, wd):
    tokens, d = x.shape
    ff = wg.shape[2]
    chunks, dchunks = ff // CHUNK, d // CHUNK
    rows, drows = wg.shape[1], wd.shape[1]
    shape = jax.ShapeDtypeStruct
    dma = pltpu.SemaphoreType.DMA
    states, turned, wide, tall = (tokens, d), (d, tokens), (side, side, rows, ff), (side, side, drows, d)
    outs = [shape((chunks, tokens, CHUNK), F32)] * 2 + [shape((chunks, tokens, CHUNK), BF16)]
    outs += [shape(s, BF16) for s in (turned, turned, states, states, turned, tall, wide, wide, tall)]
    gathers = [dma((2, chunks, 7)), dma((2, chunks, 7)), dma((2, dchunks, 7))] * 2
    return pl.pallas_call(
        functools.partial(front_kernel, side),
        name="front",
        out_shape=outs,
        in_specs=[ANY, ANY, VMEM, VMEM, VMEM],
        out_specs=[ANY] * len(outs),
        scratch_shapes=[
            *(pltpu.VMEM(s, BF16) for s in (states, states, (tokens, ff), wide, wide, tall)),
            pltpu.VMEM((2, tokens // SPAN, SPAN, CHUNK), F32),
            *(pltpu.VMEM((2, *s), BF16) for s in ((WIDE, d), (d, WIDE), (WIDE, d), (WIDE, d))),
            dma((tokens // WIDE,)),
            dma((chunks,)),
            dma((2, tokens // SPAN)),
            dma((6,)),
            *gathers,
        ],
        compiler_params=pltpu.CompilerParams(vmem_limit_bytes=VMEM_LIMIT, collective_id=0, has_side_effects=True),
        cost_estimate=pl.CostEstimate(flops=6 * tokens * d * ff, bytes_accessed=40 * tokens * d, transcendentals=tokens * ff),
    )(x, dy, wg, wu, wd)


SUBS = ((0, 0, 0, 1), (0, 1, 0, -1), (1, 0, 1, 1), (1, 1, 1, -1))


def fetch(hidden, bufs, sems, c):
    slot = lax.rem(c, bufs.shape[0])
    return local(hidden.at[c], bufs.at[slot], sems.at[slot])


class Grads:
    def __init__(self, torus, own, dwd, wide_refs, tall_refs, gg, gu, gd, slots, stages, turn):
        self.t, self.own, self.dwd, self.out, self.gd = torus, own, dwd, (gg, gu), gd
        self.rows, self.drows = gg.shape[0], gd.shape[0]
        self.wide, self.tall = Scatter(torus, self.rows, wide_refs), Scatter(torus, self.drows, tall_refs)
        self.slots, self.stages, self.turn = slots, stages, turn

    def wide_stage(self, n, c):
        slot, stage = lax.rem(c, self.slots), lax.rem(c, self.stages)
        for sub, (which, group, axis, way) in enumerate(SUBS):
            lanes = pl.ds(group * LANES, LANES)

            def own(i, j, which=which, lanes=lanes):
                return self.own[slot, which, aligned((i * self.t.side + j) * self.rows, self.rows), lanes]

            def out(value, which=which, group=group):
                self.out[which][:, aligned(c * CHUNK + group * LANES, LANES)] = value.astype(BF16)

            self.wide.stage(n, c * len(SUBS) + sub, stage * len(SUBS) + sub, axis, way, own, out)

    def earlier(self, stages, c):
        for back, n in reversed(list(enumerate(stages, 1))):

            @pl.when(c >= back)
            def _(n=n, back=back):
                self.wide_stage(n, c - back)

    def tall_gradient(self, c, chunks, turned, hidden, bufs, sems):
        @pl.when(c + 2 < chunks)
        def _():
            fetch(hidden, bufs, sems, c + 2).start()

        fetch(hidden, bufs, sems, c).wait()
        self.dwd[aligned(c * CHUNK, CHUNK), :] = dot(turned[...], bufs[lax.rem(c, bufs.shape[0])]).T

    def tall_stage(self, n):
        for k in range(self.gd.shape[1] // LANES):
            lanes = pl.ds(k * LANES, LANES)

            def own(i, j, lanes=lanes):
                return self.dwd[aligned((i * self.t.side + j) * self.drows, self.drows), lanes]

            def out(value, lanes=lanes):
                self.gd[:, lanes] = value.astype(BF16)

            self.tall.stage(n, k, k, (k + self.turn) % 2, 1 - 2 * (k // 2 % 2), own, out)


def mid_kernel(side, slots, stages, a1, a1t, dy, dyt, h, wg, wu, wd, gg, gu, gd, dh, dht, po, dgo, duo, vg, vu, vd, vdy, own, dwd, *rest):
    wide_refs, tall_refs, (lsem, esem, wsem, ssem, psem, osem) = rest[:6], rest[6:12], rest[12:]
    t = Torus(side)
    d, ff = vg.shape
    tokens = vdy.shape[0]
    chunks = ff // CHUNK
    spans = tokens // SPAN
    grads = Grads(t, own, dwd, wide_refs, tall_refs, gg, gu, gd, slots, stages, 0)

    def first(va, vat, bufs):
        def early(j):
            r = aligned(j * SPAN, SPAN)
            return [local(s.at[r], o.at[r], esem.at[i, j]) for i, (s, o) in enumerate(((a1, va), (dy, vdy)))]

        def weights(c):
            cols = aligned(c * CHUNK, CHUNK)
            views = ((wg, vg, (slice(None), cols)), (wu, vu, (slice(None), cols)), (wd, vd, (cols,)))
            return [local(s.at[at], o.at[at], wsem.at[i, c]) for i, (s, o, at) in enumerate(views)]

        turned, last = local(a1t, vat, lsem.at[0]), local(dyt, vat, lsem.at[1])

        def begin(copies):
            for c in copies:
                c.start()

        def end(copies):
            for c in copies:
                c.wait()

        begin(weights(0))
        loop(spans, lambda j: begin(early(j)))
        t.greet(greeted(t, (1, -1)))

        def stash(c, j):
            r = aligned(j * SPAN, SPAN)
            return [local(bufs.at[i, r], o.at[c, r], ssem.at[i, j]) for i, o in enumerate((dgo, duo, po))]

        def hidden(c):
            end(weights(c))

            @pl.when(c + 1 < chunks)
            def _():
                begin(weights(c + 1))

            cols = aligned(c * CHUNK, CHUNK)

            def span(j):
                @pl.when(c == 0)
                def _():
                    end(early(j))

                @pl.when(c >= 1)
                def _():
                    end(stash(c, j))

                for u in range(UNROLL):
                    r = aligned(j * SPAN + u * TILE, TILE)
                    a = va[r, :]
                    gate = dot(a, vg[:, cols])
                    up = dot(a, vu[:, cols])
                    dp = rounded(dot_nt(vdy[r, :], vd[cols, :]))
                    s = 1 / (1 + jnp.exp(-gate))
                    b = gate * s
                    bufs[2, r, :] = (b * up).astype(BF16)
                    bufs[0, r, :] = (dp * (up * (s + b * (1 - s)))).astype(BF16)
                    bufs[1, r, :] = (dp * b).astype(BF16)
                begin(stash(c, j))

                @pl.when(jnp.logical_and(c == 0, j == 0))
                def _():
                    turned.start()

            loop(spans, span)
            slot = lax.rem(c, slots)

            @pl.when(c == 0)
            def _():
                turned.wait()

            grads.earlier((1, 3), c)
            for which in BOTH:
                own[slot, which] = dot(vat[...], bufs[which])
            grads.earlier((2, 4), c)
            grads.wide_stage(0, c)

        loop(chunks, hidden)
        last.start()
        for j in range(spans):
            end(stash(0, j))

        for c in range(2):
            fetch(po, bufs, psem, c).start()
        last.wait()

        def gradient(c):
            grads.tall_gradient(c, chunks, vat, po, bufs, psem)
            for at, n, back in ((0, 3, 2), (0, 1, 1), (1, 4, 2), (2, 2, 1), (4, 3, 1), (6, 4, 1)):

                @pl.when(c == at)
                def _(n=n, back=back):
                    grads.wide_stage(n, chunks - back)

        loop(chunks, gradient)
        grads.tall_stage(0)

    pl.run_scoped(
        first,
        *(pltpu.VMEM(s, BF16) for s in ((tokens, d), (d, tokens), (3, tokens, CHUNK))),
    )

    def second(tg, tu, th, to, tt):
        blocks = tokens // WIDE

        def ins(b, s):
            r = aligned(b * WIDE, WIDE)
            return [local(src, dst.at[s], osem.at[i, s]) for i, (src, dst) in enumerate(((dgo.at[:, r], tg), (duo.at[:, r], tu), (h.at[r], th)))]

        def outs(b, s):
            r = aligned(b * WIDE, WIDE)
            return [local(src.at[s], dst, osem.at[3 + i, s]) for i, (src, dst) in enumerate(((to, dh.at[r]), (tt, dht.at[:, r])))]

        for c in ins(0, 0):
            c.start()

        def block(b):
            s = lax.rem(b, 2)

            @pl.when(b + 1 < blocks)
            def _():
                for c in ins(b + 1, 1 - s):
                    c.start()

            for at, n in ((3, 1), (5, 2), (6, 3), (7, 4)):

                @pl.when(b == at)
                def _(n=n):
                    grads.tall_stage(n)

            for c in ins(b, s):
                c.wait()

            @pl.when(b >= 2)
            def _():
                for c in outs(b - 2, s):
                    c.wait()

            r = aligned(b * WIDE, WIDE)
            sides = [jnp.concatenate([half[s, c] for c in range(chunks)], axis=1) for half in (tg, tu)]
            da = rounded(rounded(dot_nt(sides[0], vg[...])) + rounded(dot_nt(sides[1], vu[...])))
            wide = th[s].astype(F32)
            scale = scale_of(wide)
            across = jnp.sum(da * wide, -1, keepdims=True)
            dn = da * scale - wide * (across * (scale * scale * scale) / d)
            value = (vdy[r, :].astype(F32) + rounded(dn)).astype(BF16)
            to[s] = value
            tt[s] = value.T
            for c in outs(b, s):
                c.start()

        loop(blocks, block)
        for s in BOTH:
            for c in outs(s, s):
                c.wait()

    pl.run_scoped(
        second,
        *(pltpu.VMEM((2, *s), BF16) for s in ((chunks, WIDE, CHUNK), (chunks, WIDE, CHUNK), (WIDE, d), (WIDE, d), (d, WIDE))),
    )


def mid(side, rows, drows, a1, a1t, dy, dyt, h, wg, wu, wd):
    tokens, d = a1.shape
    ff = wg.shape[1]
    chunks = ff // CHUNK
    slots, stages = 2, 3
    shape = jax.ShapeDtypeStruct
    dma = pltpu.SemaphoreType.DMA
    return pl.pallas_call(
        functools.partial(mid_kernel, side, slots, stages),
        name="mid",
        out_shape=[shape(s, BF16) for s in ((rows, ff), (rows, ff), (drows, d), (tokens, d), (d, tokens), *[(chunks, tokens, CHUNK)] * 3)],
        in_specs=[ANY] * 8,
        out_specs=[VMEM] * 3 + [ANY] * 5,
        scratch_shapes=[
            *(pltpu.VMEM(s, BF16) for s in ((d, ff), (d, ff), (ff, d), (tokens, d))),
            pltpu.VMEM((slots, 2, d, CHUNK), F32),
            pltpu.VMEM((ff, d), F32),
            *Scatter.scratch(side, rows, chunks * len(SUBS), stages * len(SUBS)),
            *Scatter.scratch(side, drows, d // LANES, d // LANES),
            *(dma(s) for s in ((2,), (2, tokens // SPAN), (3, chunks), (3, tokens // SPAN), (3,), (5, 2))),
        ],
        compiler_params=pltpu.CompilerParams(vmem_limit_bytes=VMEM_LIMIT, collective_id=1, has_side_effects=True),
        cost_estimate=pl.CostEstimate(flops=16 * tokens * d * ff, bytes_accessed=40 * tokens * d, transcendentals=tokens * ff),
    )(a1, a1t, dy, dyt, h, wg, wu, wd)


def back_kernel(side, slots, stages, dh, dht, a0t, po, ao, bo, wd, g1, u1, d1, gg, gu, gd, total, vd, vdh, vdht, vat, pair, ab, own, dwd, *rest):
    wide_refs, tall_refs, (tiles, lsem, asem, psem, tsem) = rest[:6], rest[6:12], rest[12:]
    t = Torus(side)
    tokens, d = vdh.shape
    ff = vd.shape[0]
    chunks, spans = ff // CHUNK, tokens // SPAN
    depth = ab.shape[1]
    grads = Grads(t, own, dwd, wide_refs, tall_refs, gg, gu, gd, slots, stages, 1)

    def saved(step):
        c, j, slot = step // spans, lax.rem(step, spans), lax.rem(step, depth)
        return [local(s.at[c, aligned(j * SPAN, SPAN)], ab.at[i, slot], asem.at[i, slot]) for i, s in enumerate((ao, bo))]

    def begin(copies):
        for c in copies:
            c.start()

    def end(copies):
        for c in copies:
            c.wait()

    ins = [local(s, o, lsem.at[i]) for i, (s, o) in enumerate(((dht, vdht), (dh, vdh), (a0t, vat), (wd, vd)))]
    ins[0].start()
    for c in range(2):
        fetch(po, pair, psem, c).start()
    t.greet(greeted(t, range(1, side)))
    ins[0].wait()

    def gradient(c):
        @pl.when(c == 1)
        def _():
            begin(ins[1:])

        for step in range(depth - 1):

            @pl.when(c == 2 + step)
            def _(step=step):
                begin(saved(step))

        grads.tall_gradient(c, chunks, vdht, po, pair, psem)

    loop(chunks, gradient)
    grads.tall_stage(0)
    end(ins[1:])

    def hidden(c):
        cols = aligned(c * CHUNK, CHUNK)

        def span(j):
            step = c * spans + j

            @pl.when(step + depth - 1 < chunks * spans)
            def _():
                begin(saved(step + depth - 1))

            end(saved(step))
            slot = lax.rem(step, depth)
            for u in range(UNROLL):
                r = aligned(j * SPAN + u * TILE, TILE)
                mine = pl.ds(u * TILE, TILE)
                dp = rounded(dot_nt(vdh[r, :], vd[cols, :]))
                for i in BOTH:
                    pair[i, r, :] = (dp * ab[i, slot, mine, :]).astype(BF16)

        loop(spans, span)

        for n in (1, 2, 3, 4):

            @pl.when(c == n + 1)
            def _(n=n):
                grads.tall_stage(n)

        slot = lax.rem(c, slots)
        for which in BOTH:
            own[slot, which] = dot(vat[...], pair[which])
        grads.earlier((1, 2, 3, 4), c)
        grads.wide_stage(0, c)

    loop(chunks, hidden)
    for first in (1, 2, 3, 4):
        for back, n in enumerate(range(first, 5), 1):
            grads.wide_stage(n, chunks - back)

    squares = functools.reduce(lambda a, b: a + b, [jnp.sum(jnp.square(g[...].astype(F32))) for g in (g1, u1, d1, gg, gu, gd)])
    value = jnp.full(total.shape, squares, F32)
    for axis in BOTH:
        tiles[axis, 0] = value
        sent = [remote(tiles.at[axis, 0], tiles.at[axis, away], tsem.at[axis, 0, away], tsem.at[axis, 1, away], t.id(axis, away)) for away in range(1, side)]
        begin(sent)
        end(sent)
        value = functools.reduce(lambda a, b: a + b, [tiles[axis, i] for i in range(side)])
    total[...] = value


def back(side, dh, dht, a0t, po, ao, bo, wd, g1, u1, d1):
    tokens, d = dh.shape
    ff = wd.shape[0]
    rows, drows = g1.shape[0], d1.shape[0]
    chunks = ff // CHUNK
    slots, stages, depth = 3, 4, 5
    shape = jax.ShapeDtypeStruct
    dma = pltpu.SemaphoreType.DMA
    return pl.pallas_call(
        functools.partial(back_kernel, side, slots, stages),
        name="back",
        out_shape=[shape((rows, ff), BF16), shape((rows, ff), BF16), shape((drows, d), BF16), shape((8, LANES), F32)],
        in_specs=[ANY] * 7 + [VMEM] * 3,
        out_specs=[VMEM] * 4,
        scratch_shapes=[
            *(pltpu.VMEM(s, BF16) for s in ((ff, d), (tokens, d), (d, tokens), (d, tokens), (3, tokens, CHUNK))),
            pltpu.VMEM((2, depth, SPAN, CHUNK), F32),
            pltpu.VMEM((slots, 2, d, CHUNK), F32),
            pltpu.VMEM((ff, d), F32),
            *Scatter.scratch(side, rows, chunks * len(SUBS), stages * len(SUBS)),
            *Scatter.scratch(side, drows, d // LANES, d // LANES),
            pltpu.VMEM((2, side, 8, LANES), F32),
            *(dma(s) for s in ((4,), (2, depth), (3,), (2, 2, side))),
        ],
        compiler_params=pltpu.CompilerParams(vmem_limit_bytes=VMEM_LIMIT, collective_id=2, has_side_effects=True),
        cost_estimate=pl.CostEstimate(flops=8 * tokens * d * ff, bytes_accessed=40 * tokens * d, transcendentals=0),
    )(dh, dht, a0t, po, ao, bo, wd, g1, u1, d1)


def adamw(w, m, v, g):
    m = 0.9 * m + 0.1 * g
    v = 0.95 * v + 0.05 * g * g
    step = m * lax.rsqrt(v + 1e-8) + 0.1 * w
    return (w - 0.02 * step).astype(BF16), m, v


def solution(mesh):
    side = math.isqrt(mesh.shape["dp"])
    group = side * side

    def step(x, dy, *arrays):
        weights, m, v = (arrays[i : i + 3] for i in (0, 3, 6))
        wg, wu, wd = weights
        x, dy = x[0], dy[0]
        d, ff = x.shape[1], wg.shape[2]
        ao, bo, po, a0t, dyt, h, a1, a1t, wd0, wg1, wu1, wd1 = front(side, x, dy, wg, wu, wd)
        last = mid(side, wg.shape[1], wd.shape[1], a1, a1t, dy, dyt, h, wg1.reshape(d, ff), wu1.reshape(d, ff), wd1.reshape(ff, d))
        g1, dh, dht = last[:3], last[3], last[4]
        *g0, total = back(side, dh, dht, a0t, po, ao, bo, wd0.reshape(ff, d), *g1)
        count = group * sum(g.size for g in (*g0, *g1))
        factor = jnp.minimum(1.0, 0.5 * lax.rsqrt(total[0, 0] / count + 1e-30))
        new = [
            adamw(w.astype(F32), m, v, jnp.stack([first, second]).astype(F32) * factor)
            for w, m, v, first, second in zip(weights, m, v, g0, g1, strict=True)
        ]
        return tuple(one[which] for which in range(3) for one in new)

    states, cut = P(("rep", "dp"), None, None), P(None, "dp", None)
    return jax.shard_map(
        step,
        mesh=mesh,
        in_specs=(states, states) + (cut,) * 9,
        out_specs=(P("rep", "dp", None),) * 9,
        check_vma=False,
    )
```

time: 859 us -> 329 us (0.38)
  waiting for transfers between devices: 389 us -> 0 us
  matrix products: 357 us -> 0 us
  Pallas kernels: 0 us -> 319 us
  blocking collectives: 38.7 us -> 0 us
  local copies, waits for them, and re-layouts: 22.7 us -> 1.19 us
  other arithmetic: 25.4 us -> 7.21 us
  between operations: 17.2 us -> 1.36 us
    dot_general x15 -> x0, matrix products: 357 us -> none  [the longest x5 129 us: layer(): gate = jnp.dot(a, w['w_gate'], preferred_element_type=jnp.float32)]
    pallas_call x0 -> x3, Pallas kernels: none -> 319 us  [the longest x1 136 us: mid(): pl.pallas_call(functools.partial(mid_kernel, side, slots, stages), name='...]
    reduce_scatter x6 -> x0, waiting for transfers between devices: 264 us -> none  [step(): lax.psum_scatter(by_w[name], 'dp', scatter_dimension=0, tiled=True)]
    all_gather x6 -> x0, waiting for transfers between devices: 123 us -> none  [fetched(): lax.all_gather(w[number], 'dp', axis=0, tiled=True)]
    psum x1 -> x0, blocking collectives: 38.7 us -> none  [step(): squares = lax.psum(sum((jnp.sum(g * g) for g in gradients)), 'dp')]
    unnamed x28 -> x0, local copies, waits for them, and re-layouts: 17.4 us -> none
    add_any x1 -> x0, other arithmetic: 9.67 us -> none  [normed(): wide = h.astype(jnp.float32)]
    reduce_sum x4 -> x0, other arithmetic: 9.43 us -> none  [the longest x3 5.35 us: step(): squares = lax.psum(sum((jnp.sum(g * g) for g in gradients)), 'dp')]
  transfers between devices with their start and end apart: 12 -> 0, of which waited for: 10 -> 0; matrix products, arithmetic and copies ran while one was open for 40% -> 0% of each run, Pallas kernels for 0% -> 0%
where the time goes in v1:
time: 329 us
  Pallas kernels  319 us (97%)
  other arithmetic  7.21 us (2%)
    pallas_call x1, Pallas kernels, mid(): pl.pallas_call(functools.partial(mid_kernel, side, slots, stages), name='...  136 us
    pallas_call x1, Pallas kernels, back(): pl.pallas_call(functools.partial(back_kernel, side, slots, stages), name=...  95.4 us
    pallas_call x1, Pallas kernels, front(): pl.pallas_call(functools.partial(front_kernel, side), name='front', out_s...  87.6 us
    convert_element_type x2, other arithmetic, adamw(): return ((w - 0.02 * step).astype(BF16), m, v)  7.21 us

profile of v1, /device:TPU:96, one launch (start us, length us, event | category | flops | bytes accessed | tf_op | source)
XLA Modules:
  0.0 328.9 jit_solution(12916407243184249330)
XLA Ops:
  0.6 87.6 %front.1 = (f32[7,4096,256]{2,1,0:T(8,128)}, f32[7,4096,256]{2,1,0:T(8,128)}, bf16[7,4096,256]{2,1,0:T(8,128)(2,1)}, bf16[768,4096]{1,0:T(8,128)(2,1)}, bf16[768...) custom-call(bf16[4096,768]{1,0:T(8,128)(2,1)} %bitcast.19, ...), custom_call_target="tpu_custom_call" | custom-call | flops 33822867456 | bytes 125829120 | tf_op jit(solution)/shard_map/front/pallas_call | solution.py:419
  88.2 136.1 %mid.1 = (bf16[48,1792]{1,0:T(8,128)(2,1)}, bf16[48,1792]{1,0:T(8,128)(2,1)}, bf16[112,768]{1,0:T(8,128)(2,1)}, bf16[4096,768]{1,0:T(8,128)(2,1)}, bf16[768,4096...) custom-call(bf16[4096,768]{1,0:T(8,128)(2,1)} %get-tuple-element.30., ...), custom_call_target="tpu_custom_call" | custom-call | flops 90194313216 | bytes 125829120 | tf_op jit(solution)/shard_map/mid/pallas_call | solution.py:673
  224.4 95.4 %back.1 = (bf16[48,1792]{1,0:T(8,128)(2,1)}, bf16[48,1792]{1,0:T(8,128)(2,1)}, bf16[112,768]{1,0:T(8,128)(2,1)}, f32[8,128]{1,0:T(8,128)}) custom-call(bf16[4096,768]{1,0:T(8,128)(2,1)} %get-tuple-element.37.dh, bf16[768,4096]{1,0:T(8,128)(2,1)} %get-tuple-element.38.dht, bf16[768,4096]{1,0:T(8,128)(2,1)} %get-tuple-element.39.a0t, ...), custom_call_target="tpu_custom_call" | custom-call | flops 45097156608 | bytes 125829120 | tf_op jit(solution)/shard_map/back/pallas_call | solution.py:794
  319.8 1.2 slice.3
  321.7 2.9 fusion.8
  324.6 4.3 %fusion.2 = (bf16[2,48,1792]{2,1,0:T(8,128)(2,1)}, f32[2,48,1792]{2,1,0:T(8,128)}, f32[2,48,1792]{2,1,0:T(8,128)}, bf16[2,48,1792]{2,1,0:T(8,128)(2,1)}, f32[2,48,1792]{2,1,0:T(8,128)}, /*index=5*/f32[2,48,1792]{2,1,0:T(8,128)}) fusion(bf16[2,48,1792]{2,1,0:T(8,128)(2,1)} %wg.1, f32[]{:T(128)} %bitcast.8, bf16[1,48,1792]{2,1,0:T(8,128)(2,1)} %bitcast.15, ...), kind=kLoop, calls=%fused_computation.11 | loop fusion | flops 6881280 | bytes 7569412 | tf_op jit(solution)/shard_map/convert_element_type | solution.py:819

commit v2 on v1

--- a/solution.py
+++ b/solution.py
@@ -327,12 +327,7 @@
         return local(vp.at[:, aligned(c * CHUNK, CHUNK)], po.at[c], psem.at[c])
 
     def hidden(c):
-        for n in (3, 4, 5):
-
-            @pl.when(c + (5 - n) < chunks)
-            def _(n=n):
-                wide(0, n, c + (5 - n))
-
+        wide(0, 5, c)
         due(c, ((0, (tall, 0, 1), (all_wide, 1, 0)), (1, (tall, 0, 2)), (2, (tall, 0, 3), (all_wide, 1, 1)), (3, (tall, 1, 0))))
         due(c, ((4, (tall, 0, 4), (all_wide, 1, 2)), (5, (tall, 1, 1)), (6, (tall, 1, 2), (all_wide, 1, 3))))
         cols = aligned(c * CHUNK, CHUNK)
@@ -356,6 +351,12 @@
                 vp[r, cols] = (b * up).astype(BF16)
             for copy in saved(c, j):
                 copy.start()
+
+            for ahead, n in ((1, 4), (2, 3)):
+
+                @pl.when(jnp.logical_and(j == ahead, c + ahead < chunks))
+                def _(ahead=ahead, n=n):
+                    wide(0, n, c + ahead)
 
         loop(spans, span)
         kept(c).start()
@@ -480,8 +481,16 @@
         fetch(hidden, bufs, sems, c).wait()
         self.dwd[aligned(c * CHUNK, CHUNK), :] = dot(turned[...], bufs[lax.rem(c, bufs.shape[0])]).T
 
-    def tall_stage(self, n):
-        for k in range(self.gd.shape[1] // LANES):
+    def tall_pairs(self, i, starts, waits):
+        for pair in range(starts):
+            for n, wait in enumerate(waits):
+
+                @pl.when(i == pair + wait)
+                def _(n=n, pair=pair):
+                    self.tall_stage(n, pair)
+
+    def tall_stage(self, n, pair):
+        for k in (2 * pair, 2 * pair + 1):
             lanes = pl.ds(k * LANES, LANES)
 
             def own(i, j, lanes=lanes):
@@ -596,7 +605,6 @@
                     grads.wide_stage(n, chunks - back)
 
         loop(chunks, gradient)
-        grads.tall_stage(0)
 
     pl.run_scoped(
         first,
@@ -605,6 +613,7 @@
 
     def second(tg, tu, th, to, tt):
         blocks = tokens // WIDE
+        pairs, waits = d // CHUNK, (0, 2, 4, 5, 6)
 
         def ins(b, s):
             r = aligned(b * WIDE, WIDE)
@@ -625,11 +634,7 @@
                 for c in ins(b + 1, 1 - s):
                     c.start()
 
-            for at, n in ((3, 1), (5, 2), (6, 3), (7, 4)):
-
-                @pl.when(b == at)
-                def _(n=n):
-                    grads.tall_stage(n)
+            grads.tall_pairs(b, pairs, waits)
 
             for c in ins(b, s):
                 c.wait()
@@ -653,6 +658,11 @@
                 c.start()
 
         loop(blocks, block)
+        for i in range(blocks, pairs + waits[-1]):
+            for pair in range(pairs):
+                for n, wait in enumerate(waits):
+                    if i == pair + wait:
+                        grads.tall_stage(n, pair)
         for s in BOTH:
             for c in outs(s, s):
                 c.wait()
@@ -731,7 +741,6 @@
         grads.tall_gradient(c, chunks, vdht, po, pair, psem)
 
     loop(chunks, gradient)
-    grads.tall_stage(0)
     end(ins[1:])
 
     def hidden(c):
@@ -755,11 +764,7 @@
 
         loop(spans, span)
 
-        for n in (1, 2, 3, 4):
-
-            @pl.when(c == n + 1)
-            def _(n=n):
-                grads.tall_stage(n)
+        grads.tall_pairs(c, d // CHUNK, range(5))
 
         slot = lax.rem(c, slots)
         for which in BOTH:
@@ -819,6 +824,30 @@
     return (w - 0.02 * step).astype(BF16), m, v
 
 
+def step_kernel(count, total, *refs):
+    ws, ms, vs, firsts, seconds = (refs[i : i + 3] for i in range(0, 15, 3))
+    outs = refs[15:]
+    factor = jnp.minimum(1.0, 0.5 * lax.rsqrt(total[0:1, 0:1] / count + 1e-30))
+    for i, (w, m, v, first, second) in enumerate(zip(ws, ms, vs, firsts, seconds)):
+        for layer, g in enumerate((first, second)):
+            new = adamw(w[layer].astype(F32), m[layer], v[layer], g[...].astype(F32) * factor)
+            for which, value in enumerate(new):
+                outs[3 * which + i][layer] = value
+
+
+def updated(count, total, weights, m, v, firsts, seconds):
+    shape = jax.ShapeDtypeStruct
+    outs = [shape(w.shape, dtype) for dtype in (BF16, F32, F32) for w in weights]
+    return pl.pallas_call(
+        functools.partial(step_kernel, count),
+        name="adamw",
+        out_shape=outs,
+        in_specs=[VMEM] * 16,
+        out_specs=[VMEM] * len(outs),
+        compiler_params=pltpu.CompilerParams(vmem_limit_bytes=VMEM_LIMIT // 2),
+    )(total, *weights, *m, *v, *firsts, *seconds)
+
+
 def solution(mesh):
     side = math.isqrt(mesh.shape["dp"])
     group = side * side
@@ -833,12 +862,7 @@
         g1, dh, dht = last[:3], last[3], last[4]
         *g0, total = back(side, dh, dht, a0t, po, ao, bo, wd0.reshape(ff, d), *g1)
         count = group * sum(g.size for g in (*g0, *g1))
-        factor = jnp.minimum(1.0, 0.5 * lax.rsqrt(total[0, 0] / count + 1e-30))
-        new = [
-            adamw(w.astype(F32), m, v, jnp.stack([first, second]).astype(F32) * factor)
-            for w, m, v, first, second in zip(weights, m, v, g0, g1, strict=True)
-        ]
-        return tuple(one[which] for which in range(3) for one in new)
+        return tuple(updated(count, total, weights, m, v, g0, g1))
 
     states, cut = P(("rep", "dp"), None, None), P(None, "dp", None)
     return jax.shard_map(

time: 329 us -> 342 us (1.040)
  local copies, waits for them, and re-layouts: 1.19 us -> 15.7 us
  other arithmetic: 7.21 us -> 0 us
  Pallas kernels: 319 us -> 325 us
    unnamed x0 -> x32, local copies, waits for them, and re-layouts: none -> 15.7 us
    convert_element_type x2 -> x0, other arithmetic: 7.21 us -> none  [adamw(): return ((w - 0.02 * step).astype(BF16), m, v)]
    pallas_call x0 -> x1, Pallas kernels: none -> 3.55 us  [updated(): pl.pallas_call(functools.partial(step_kernel, count), name='adamw', out_s...]
where the time goes in v2:
time: 342 us; the launch traced here: 341 us
  Pallas kernels  325 us (95%)
  local copies, waits for them, and re-layouts  15.7 us (5%)
    pallas_call x1, Pallas kernels, mid(): pl.pallas_call(functools.partial(mid_kernel, side, slots, stages), name='...  134 us
    pallas_call x1, Pallas kernels, back(): pl.pallas_call(functools.partial(back_kernel, side, slots, stages), name=...  96.3 us
    pallas_call x1, Pallas kernels, front(): pl.pallas_call(functools.partial(front_kernel, side), name='front', out_s...  90.8 us
    unnamed x32, local copies, waits for them, and re-layouts  15.7 us

profile of v2, /device:TPU:96, one launch (start us, length us, event | category | flops | bytes accessed | tf_op | source)
XLA Modules:
  0.0 341.4 jit_solution(17652972378606243039)
XLA Ops:
  0.6 90.8 %front.1 = (f32[7,4096,256]{2,1,0:T(8,128)}, f32[7,4096,256]{2,1,0:T(8,128)}, bf16[7,4096,256]{2,1,0:T(8,128)(2,1)}, bf16[768,4096]{1,0:T(8,128)(2,1)}, bf16[768...) custom-call(bf16[4096,768]{1,0:T(8,128)(2,1)} %bitcast.6, ...), custom_call_target="tpu_custom_call" | custom-call | flops 33822867456 | bytes 125829120 | tf_op jit(solution)/shard_map/front/pallas_call | solution.py:420
  91.4 134.3 %mid.1 = (bf16[48,1792]{1,0:T(8,128)(2,1)}, bf16[48,1792]{1,0:T(8,128)(2,1)}, bf16[112,768]{1,0:T(8,128)(2,1)}, bf16[4096,768]{1,0:T(8,128)(2,1)}, bf16[768,4096...) custom-call(bf16[4096,768]{1,0:T(8,128)(2,1)} %get-tuple-element.30., ...), custom_call_target="tpu_custom_call" | custom-call | flops 90194313216 | bytes 125829120 | tf_op jit(solution)/shard_map/mid/pallas_call | solution.py:683
  225.8 96.3 %back.1 = (bf16[48,1792]{1,0:T(8,128)(2,1)}, bf16[48,1792]{1,0:T(8,128)(2,1)}, bf16[112,768]{1,0:T(8,128)(2,1)}, f32[8,128]{1,0:T(8,128)}) custom-call(bf16[4096,768]{1,0:T(8,128)(2,1)} %get-tuple-element.37.dh, bf16[768,4096]{1,0:T(8,128)(2,1)} %get-tuple-element.38.dht, bf16[768,4096]{1,0:T(8,128)(2,1)} %get-tuple-element.39.a0t, ...), custom_call_target="tpu_custom_call" | custom-call | flops 45097156608 | bytes 125829120 | tf_op jit(solution)/shard_map/back/pallas_call | solution.py:799
  322.1 0.0 copy-start
  322.1 1.1 copy-done
  323.2 0.0 copy-start.1
  323.2 1.1 copy-done.1
  324.3 0.0 copy-start.2
  324.3 1.1 copy-done.2
  325.4 0.0 copy-start.3
  325.4 1.1 copy-done.3
  326.5 0.0 copy-start.4
  326.5 1.1 copy-done.4
  327.6 0.0 copy-start.5
  327.6 1.1 copy-done.5
  328.7 0.0 copy-start.6
  328.7 1.0 copy-done.6
  329.7 0.0 copy-start.7
  329.7 1.0 copy-done.7
  330.7 0.0 copy-start.8
  330.7 1.0 copy-done.8
  331.6 0.0 copy-start.9
  331.6 0.9 copy-done.9
  332.6 0.0 copy-start.10
  332.6 0.9 copy-done.10
  333.5 0.0 copy-start.11
  333.5 0.9 copy-done.11
  334.4 0.0 copy-start.12
  334.4 0.9 copy-done.12
  335.3 0.0 copy-start.13
  335.3 0.9 copy-done.13
  336.2 0.0 copy-start.14
  336.2 0.9 copy-done.14
  337.2 0.0 copy-start.15
  337.2 0.7 copy-done.15
  337.8 3.6 %adamw.1 = (bf16[2,48,1792]{2,1,0:T(8,128)(2,1)}, bf16[2,48,1792]{2,1,0:T(8,128)(2,1)}, bf16[2,112,768]{2,1,0:T(8,128)(2,1)}, f32[2,48,1792]{2,1,0:T(8,128)}, f3...) custom-call(f32[8,128]{1,0:T(8,128)S(1)} %copy-done.15, ...), custom_call_target="tpu_custom_call" | custom-call | tf_op jit(solution)/shard_map/adamw/pallas_call | solution.py:841
Async XLA Ops:
  322.1 1.1 copy-start
  323.2 1.1 copy-start.1
  324.3 1.1 copy-start.2
  325.4 1.1 copy-start.3
  326.5 1.1 copy-start.4
  327.6 1.1 copy-start.5
  328.7 1.0 copy-start.6
  329.7 1.0 copy-start.7
  330.7 1.0 copy-start.8
  331.6 0.9 copy-start.9
  332.6 0.9 copy-start.10
  333.5 0.9 copy-start.11
  334.4 0.9 copy-start.12
  335.3 0.9 copy-start.13
  336.2 0.9 copy-start.14
  337.2 0.7 copy-start.15
